TPU v7x, 128 devices: a whole 4x4x4 slice. The times are simulated.
128 devices in a mesh: dp: 1, tp: 2 (over core), sp: 64 (over z, y, x).
Axes of the slice: x: 4, y: 4, z: 4, core: 2. Of those that a mesh axis runs over, the one named last changes fastest.
Arguments:
- hidden: bfloat16 [32, 6144], P('dp')
- norm_scale: bfloat16 [6144], replicated
- w_qkv: bfloat16 [6144, 8192], P(None, 'tp')
- w_out: bfloat16 [6144, 6144], P('tp')
- k_cache: bfloat16 [32, 4096, 8, 128], P('dp', 'sp', 'tp')
- v_cache: bfloat16 [32, 4096, 8, 128], P('dp', 'sp', 'tp')
- positions: int32 [32], P('dp')
Outputs:
- output 1: bfloat16 [32, 6144], P('dp')
- output 2: bfloat16 [32, 4096, 8, 128], P('dp', 'sp', 'tp')
- output 3: bfloat16 [32, 4096, 8, 128], P('dp', 'sp', 'tp')
All inputs are finite; a program needn't handle non-finite values.
Results may differ from a plain program's by a relative error of at most 0.00522225.
Values sent between devices are 32-bit elements.
A program may use at most 1 GiB of HBM per device.

v0:
```python
import itertools
import math

import jax
import jax.numpy as jnp
import numpy as np
from jax import lax
from jax.experimental import pallas as pl
from jax.experimental.pallas import tpu as pltpu
from jax.sharding import PartitionSpec as P

MESH = pl.DeviceIdType.MESH
VMEM = pltpu.VMEM
F32 = jnp.float32
BF16 = jnp.bfloat16
NEG = -3.0e38
PLANE = 16
K_CHUNKS = 6
KV = 4
OWNERS = 8
TURNS = (2, 1, 3, 0)
QUARTERS = (0, 1, 3, 2)
RS_ROWS = 14
AG_ROWS = 12


def farthest_first(dims):
    near = lambda o: sum(min(v, 4 - v) for v in o)
    return sorted((o for o in itertools.product(range(4), repeat=dims) if any(o)), key=lambda o: -near(o))


PLANE_ORDER = farthest_first(2)
CUBE_ORDER = farthest_first(3)


def step_kernel(pos_hbm, h_hbm, scale_hbm, freq_hbm, wq_ref, wo_ref, k_ref, v_ref, out_ref, k_buf, v_buf,
                pos_ref, h_ref, scale_ref, freq_ref, in_sem,
                wq_buf, wk_buf, wl_buf, wo_buf, recv, kvs, xs, xb, part, parts, lhs, mine, shares, full, other,
                wq_sem, wk_sem, wl_sem, wo_sem, kv_sem, q_send, q_recv, early_send, early_recv, late_send, late_recv,
                rs_send, rs_recv, x_send, x_recv, ag_send, ag_recv, tp_send, tp_recv, ready):
    sp = lax.axis_index("sp")
    tp = lax.axis_index("tp")
    n_sp = 64
    line, group = lax.div(sp, KV), lax.rem(sp, KV)
    n_lines = n_sp // KV
    j = lax.rem(sp, PLANE)
    base = sp - j
    y_at, x_at = lax.div(j, 4), lax.rem(j, 4)
    z_at = lax.div(sp, PLANE)
    is_kv = x_at == 3
    n_seq, d_model = h_ref.shape
    width = wk_buf.shape[1]
    rows = d_model // K_CHUNKS
    n_rows = k_ref.shape[1]
    seq_local = n_rows // KV
    depth = wo_buf.shape[0]
    own = d_model // OWNERS
    n_cb = own // 128

    def turn_of(dz):
        return jnp.where(dz == 2, 0, jnp.where(dz == 1, 1, jnp.where(dz == 3, 2, 3)))

    wq_at = pl.multiple_of(y_at * 1024 + 256 + x_at * 128, 128)

    def wq_copy(c):
        return pltpu.make_async_copy(
            wq_ref.at[pl.ds(c * rows, rows), pl.ds(wq_at, 128)], wq_buf.at[pl.ds(c * rows, rows)], wq_sem.at[c])

    wk_copy = pltpu.make_async_copy(
        wq_ref.at[:, pl.ds(pl.multiple_of(y_at * 1024 + 768, 256), width)], wk_buf, wk_sem)

    def wl_copy(g):
        return pltpu.make_async_copy(
            wq_ref.at[:, pl.ds(g * 1024, 256)], wl_buf.at[g // 2, :, pl.ds(g % 2 * 256, 256)], wl_sem.at[g])

    def wo_copy(k):
        return pltpu.make_async_copy(
            wo_ref.at[pl.ds(pl.multiple_of(group * depth, depth) + k * (depth // KV), depth // KV)],
            wo_buf.at[pl.ds(k * (depth // KV), depth // KV)], wo_sem.at[k])

    k_copy = pltpu.make_async_copy(k_ref, k_buf, kv_sem.at[0])
    v_copy = pltpu.make_async_copy(v_ref, v_buf, kv_sem.at[1])
    small = [pltpu.make_async_copy(src, dst, in_sem.at[i]) for i, (src, dst) in enumerate(
        [(h_hbm, h_ref), (pos_hbm, pos_ref), (freq_hbm, freq_ref), (scale_hbm, scale_ref)])]
    for c in small:
        c.start()
    barrier = pltpu.get_barrier_semaphore()

    with jax.named_scope("greet"):
        for dy, dx in PLANE_ORDER:
            peer = base + lax.rem(y_at + dy, 4) * 4 + lax.rem(x_at + dx, 4)
            pl.semaphore_signal(barrier, inc=1, device_id={"sp": peer}, device_id_type=MESH)
        for dz in range(1, 4):
            pl.semaphore_signal(barrier, inc=1, device_id={"sp": lax.rem(sp + dz * PLANE, n_sp)}, device_id_type=MESH)
        pl.semaphore_signal(barrier, inc=1, device_id={"tp": 1 - tp}, device_id_type=MESH)
        for c in range(K_CHUNKS):
            wq_copy(c).start()
        pl.when(is_kv)(wk_copy.start)

    with jax.named_scope("hwait"):
        small[0].wait()
    with jax.named_scope("norm"):
        hidden = h_ref[...].astype(F32)
        centered = hidden - jnp.mean(hidden, axis=-1, keepdims=True)
        var = jnp.mean(centered * centered, axis=-1, keepdims=True)
    with jax.named_scope("inwait"):
        for c in small[1:]:
            c.wait()
        for g in range(KV):
            wl_copy(g).start()
    with jax.named_scope("norm2"):
        u = (centered * lax.rsqrt(var + 1e-5) * scale_ref[...].astype(F32)[None, :]).astype(BF16)
        seq_row = lax.broadcasted_iota(jnp.int32, (n_seq, 128), 0)
        pos = jnp.zeros((n_seq, 128), jnp.int32)
        for b in range(n_seq):
            pos = jnp.where(seq_row == b, pos_ref[b], pos)
        angles = pos.astype(F32) * freq_ref[...]
        cos = jnp.cos(angles)
        sin = jnp.sin(angles)
        sin = jnp.where(lax.broadcasted_iota(jnp.int32, (n_seq, 128), 1) < 64, -sin, sin)

    def clipped(product):
        return jnp.clip(product.astype(BF16), -8.0, 8.0).astype(F32)

    def rotate(piece):
        return (piece * cos + pltpu.roll(piece, 64, 1) * sin).astype(BF16).astype(F32)

    def tile_of(y, z):
        return jnp.concatenate([y[z * 4:z * 4 + 4], y[16 + z * 4:16 + z * 4 + 4]], axis=0)

    with jax.named_scope("qkv"):
        accs = [jnp.zeros((n_seq, 128), F32)] * 2
        for c in range(K_CHUNKS):
            wq_copy(c).wait()
            accs[c % 2] += jnp.dot(u[:, c * rows:(c + 1) * rows], wq_buf[c * rows:(c + 1) * rows, :],
                                   preferred_element_type=F32)
        y = rotate(clipped(accs[0] + accs[1]))
        for z in range(4):
            recv[j, turn_of(lax.rem(z + 4 - z_at, 4))] = tile_of(y, z)
    with jax.named_scope("barrier"):
        pl.semaphore_wait(barrier, PLANE - 1 + 3 + 1)

    def to_plane(dy, dx, block, send_sem, recv_sem):
        peer = base + lax.rem(y_at + dy, 4) * 4 + lax.rem(x_at + dx, 4)
        return pltpu.make_async_remote_copy(
            src_ref=block, dst_ref=block, send_sem=send_sem, recv_sem=recv_sem,
            device_id={"sp": peer}, device_id_type=MESH)

    def wait_for(n, sem):
        pltpu.make_async_copy(kvs.at[pl.ds(0, n)], kvs.at[pl.ds(0, n)], sem).wait()

    def wait_for_halves(n, sem):
        flat_half = xs.at[pl.ds(0, n * n_seq // 2)]
        pltpu.make_async_copy(flat_half, flat_half, sem).wait()

    is_last = jnp.logical_and(is_kv, y_at == 3)
    with jax.named_scope("qsend"):
        for half in range(2):
            for dy, dx in PLANE_ORDER:
                to_plane(dy, dx, recv.at[j, pl.ds(half * 2, 2)], q_send, q_recv.at[half]).start()
        for dz in range(1, 4):
            pl.semaphore_signal(ready, inc=1, device_id={"sp": lax.rem(sp + dz * PLANE, n_sp)}, device_id_type=MESH)
        for g in range(KV):
            for r in (6, 7):
                xs[pl.ds(g * 8 + r, n_seq, stride=32), :] = jnp.zeros((n_seq, 128), F32)

    with jax.named_scope("newkv"):
        @pl.when(is_kv)
        def _():
            wk_copy.wait()
            y = clipped(jnp.dot(u, wk_buf[...], preferred_element_type=F32))
            y = jnp.concatenate([rotate(y[:, :128]), y[:, 128:]], axis=1)
            for z in range(4):
                kvs[y_at, turn_of(lax.rem(z + 4 - z_at, 4))] = tile_of(y, z)
            for dy in (2, 1, 3, 0):
                @pl.when(jnp.logical_or(dy != 0, y_at != 3))
                def _():
                    to_plane(dy, lax.rem(y_at + 1, 4), kvs.at[y_at], early_send, early_recv).start()

    with jax.named_scope("local"):
        for pair in range(2):
            wl_copy(pair * 2).wait()
            wl_copy(pair * 2 + 1).wait()
            if pair == 0:
                k_copy.start()
                v_copy.start()
            y = clipped(jnp.dot(u, wl_buf[pair], preferred_element_type=F32))
            for i in range(4):
                piece = rotate(y[:, i * 128:(i + 1) * 128])
                for z in range(4):
                    at = turn_of(lax.rem(z + 4 - z_at, 4)) * 256 + (pair * 2 + i // 2) * 8 + i % 2
                    xs[pl.ds(at, 8, stride=32), :] = tile_of(piece, z)
        for k in range(KV):
            wo_copy(k).start()

    def half_queries(half):
        with jax.named_scope(f"qwait{half}"):
            wait_for_halves(PLANE - 1, q_recv.at[half])
        with jax.named_scope("spread"):
            for turn in (half * 2, half * 2 + 1):
                for blk in range(PLANE):
                    xs[pl.ds(turn * 256 + blk // 4 * 8 + 2 + blk % 4, 8, stride=32), :] = recv[blk, turn]
                xb[turn * 256:(turn + 1) * 256, :] = xs[turn * 256:(turn + 1) * 256, :].astype(BF16)

    row8 = lax.broadcasted_iota(jnp.int32, (32, 128), 0) % 8
    lane32 = lax.broadcasted_iota(jnp.int32, (32, 128), 1)

    def as_rows(cols, n):
        tiles = sum(jnp.where((lane32 == row8 + 8 * t)[:8 * n], c, 0.0) for t, c in enumerate(cols)).reshape(n, 8, 128)
        return jnp.broadcast_to(jnp.sum(tiles, axis=1, keepdims=True), (n, 8, 128)).reshape(8 * n, 128)

    with jax.named_scope("kvwait"):
        k_copy.wait()
        v_copy.wait()
    row = lax.broadcasted_iota(jnp.int32, (32, n_rows), 0)
    col = lax.broadcasted_iota(jnp.int32, (32, n_rows), 1)
    seq_of = jnp.where(col % KV == row // 8, col // KV + sp * seq_local, 1 << 30)
    scale = 128 ** -0.5

    def line_at(turn, i):
        return lax.rem(z_at + TURNS[turn], 4) * 4 + lax.rem(y_at + TURNS[i], 4)

    def scores(turn):
        out = []
        for i in range(4):
            for t in range(2):
                at = (turn * 8 + t * 4 + lax.rem(y_at + TURNS[i], 4)) * 32
                b = line_at(turn, i) + 16 * t
                q = xb[pl.ds(pl.multiple_of(at, 32), 32), :]
                s = lax.dot_general(q, k_buf[b], (((1,), (1,)), ((), ())), preferred_element_type=F32) * scale
                out.append(jnp.where(seq_of < pos_ref[b], s, NEG))
        return out

    def values(turn, held):
        for i in range(4):
            ln = line_at(turn, i)
            stats, outs = [], []
            for t in range(2):
                s = held[i * 2 + t]
                m = jnp.max(s, axis=1, keepdims=True)
                e = jnp.exp(s - m)
                stats.append((m, jnp.sum(e, axis=1, keepdims=True)))
                outs.append(jnp.dot(e.astype(BF16), v_buf[ln + 16 * t], preferred_element_type=F32))
            (m0, l0), (m1, l1) = stats
            first = jnp.where(row8 == 6, as_rows((m0, m1), KV), jnp.where(row8 == 7, as_rows((l0, l1), KV), outs[0]))
            for g in range(KV):
                at = pl.multiple_of((ln * KV + g) * 16, 16)
                part[pl.ds(at, 8), :] = first[g * 8:(g + 1) * 8]
                part[pl.ds(at + 8, 8), :] = outs[1][g * 8:(g + 1) * 8]

    def send_partials(turn):
        for i in range(4):
            ln = line_at(turn, i)
            for d in TURNS:
                if turn == 3 and i == 3 and d == 0:
                    continue
                to = lax.rem(group + d, KV)
                pltpu.make_async_remote_copy(
                    src_ref=part.at[pl.ds(pl.multiple_of((ln * KV + to) * 16, 16), RS_ROWS)],
                    dst_ref=parts.at[pl.ds(pl.multiple_of(sp * 16, 16), RS_ROWS)], send_sem=rs_send,
                    recv_sem=rs_recv, device_id={"sp": ln * KV + to}, device_id_type=MESH).start()

    half_queries(0)
    with jax.named_scope("ready"):
        pl.semaphore_wait(ready, 3)
    with jax.named_scope("attn0"):
        held = scores(0)
        ahead = scores(1)
        values(0, held)
        send_partials(0)
        values(1, ahead)
        send_partials(1)
    half_queries(1)
    with jax.named_scope("attn1"):
        held = scores(2)
        ahead = scores(3)
        values(2, held)
        send_partials(2)
        values(3, ahead)
        send_partials(3)
        parts[pl.ds(pl.multiple_of(sp * 16, 16), 16), :] = part[pl.ds(pl.multiple_of(sp * 16, 16), 16), :]

    with jax.named_scope("newrow"):
        @pl.when(jnp.logical_not(is_last))
        def _():
            wait_for(1, early_recv)

        for i in range(2):
            xs[pl.ds(3 * 256 + group * 8 + 6 + i, 8, stride=32), :] = kvs[group, 3, :, i * 128:(i + 1) * 128]
        cols, v_new = [], []
        for t in range(2):
            tile = xs[pl.ds(pl.multiple_of((24 + t * 4 + y_at) * 32 + group * 8, 8), 8), :]
            cols.append(jnp.sum(tile * tile[6:7, :], axis=1, keepdims=True) * scale)
            v_new.append(tile[7:8, :])
        m_new = as_rows(cols, 1)[:1]

    rs_others = parts.at[pl.ds(0, (n_sp - 1) * RS_ROWS)]
    with jax.named_scope("rswait"):
        pltpu.make_async_copy(rs_others, rs_others, rs_recv).wait()

    with jax.named_scope("merge"):
        lane = lax.broadcasted_iota(jnp.int32, (1, 128), 1)
        m = parts[pl.ds(6, n_sp, stride=16), :]
        l = parts[pl.ds(7, n_sp, stride=16), :]
        top = jnp.maximum(jnp.max(m, axis=0, keepdims=True), m_new)
        f = jnp.exp(m - top)
        f_new = jnp.exp(m_new - top)
        real = jnp.logical_and(lane < 16, lane % 8 < 6)
        den = jnp.where(real, jnp.sum(f * l, axis=0, keepdims=True) + f_new, 1.0)
        wt = (jnp.concatenate([f, jnp.broadcast_to(f_new, (8, 128))], axis=0) / den).T
        lhs[...] = jnp.zeros_like(lhs)
        for t in range(2):
            w8 = wt[t * 8:(t + 1) * 8]
            sums = [w8[:, n_sp:n_sp + 1] * v_new[t]] + [jnp.zeros((8, 128), F32)] * 3
            for s in range(n_sp):
                sums[s % 4] += w8[:, s:s + 1] * parts[s * 16 + t * 8:s * 16 + t * 8 + 8, :]
            acc = (sums[0] + sums[1]) + (sums[2] + sums[3])
            for hd in range(6):
                lhs[t:t + 1, hd * 128:(hd + 1) * 128] = acc[hd:hd + 1, :]

    me = group * 2 + tp
    with jax.named_scope("wout"):
        for k in range(KV):
            wo_copy(k).wait()
        left = lhs[...].astype(BF16)

        order = [(dg, dt) for dg in TURNS for dt in (1, 0)]

        def product(k):
            owner = lax.rem(group + order[k][0], KV) * 2 + (1 - tp if order[k][1] else tp)
            at = pl.multiple_of(owner * own, own)
            return owner, jnp.dot(left, wo_buf[:, pl.ds(at, own)], preferred_element_type=F32)

        held = product(0)
        for k in range(OWNERS):
            ahead = product(k + 1) if k + 1 < OWNERS else None
            owner, res = held
            buf = mine if k < OWNERS - 1 else shares
            at = pl.multiple_of(owner * 16, 16)
            for t in range(2):
                for cb in range(n_cb):
                    buf[pl.ds(at + t * n_cb + cb, 1), :] = res[t:t + 1, cb * 128:(cb + 1) * 128]
            if k < OWNERS - 1:
                pltpu.make_async_remote_copy(
                    src_ref=mine.at[pl.ds(at, AG_ROWS)],
                    dst_ref=shares.at[pl.ds(pl.multiple_of(me * 16, 16), AG_ROWS)], send_sem=x_send, recv_sem=x_recv,
                    device_id={"tp": lax.rem(owner, 2), "sp": line * KV + lax.div(owner, 2)},
                    device_id_type=MESH).start()
            held = ahead

    with jax.named_scope("forward"):
        for dx in (2, 1, 3):
            to = lax.rem(x_at + dx, 4)

            @pl.when(jnp.logical_or(to != 3, y_at != x_at))
            def _():
                pltpu.make_async_remote_copy(
                    src_ref=kvs.at[group], dst_ref=kvs.at[group], send_sem=late_send,
                    recv_sem=late_recv, device_id={"sp": line * 4 + to}, device_id_type=MESH).start()

    x_others = shares.at[pl.ds(0, (OWNERS - 1) * AG_ROWS)]
    quarter_rows = n_lines * 16
    slot = pl.multiple_of((group * n_lines + line) * 16, 16)
    mine_rows = full.at[pl.ds(slot, AG_ROWS)]

    with jax.named_scope("xwait"):
        pltpu.make_async_copy(x_others, x_others, x_recv).wait()
    with jax.named_scope("agsend"):
        total = shares[0:16, :]
        for s in range(1, OWNERS):
            total += shares[s * 16:(s + 1) * 16, :]
        full[pl.ds(slot, 16), :] = total
        zs = [lax.rem(z_at + d, 4) * 16 for d in range(4)]
        ys = [lax.rem(y_at + d, 4) * 4 for d in range(4)]
        xs_ = [lax.rem(x_at + d, 4) for d in range(4)]
        for dz, dy, dx in CUBE_ORDER:
            pltpu.make_async_remote_copy(
                src_ref=mine_rows, dst_ref=mine_rows, send_sem=ag_send, recv_sem=ag_recv.at[group],
                device_id={"sp": zs[dz] + ys[dy] + xs_[dx]}, device_id_type=MESH).start()

    with jax.named_scope("latewait"):
        @pl.when(jnp.logical_and(is_kv, jnp.logical_not(is_last)))
        def _():
            wait_for(2, late_recv)

        @pl.when(jnp.logical_or(jnp.logical_not(is_kv), is_last))
        def _():
            wait_for(3, late_recv)
    with jax.named_scope("update"):
        sub = lax.broadcasted_iota(jnp.int32, (8, 128), 0)

        def update(turn, carry):
            dz = jnp.where(turn == 0, 2, jnp.where(turn == 1, 1, jnp.where(turn == 2, 3, 0)))
            for t in range(2):
                for y in range(4):
                    b = t * 16 + lax.rem(z_at + dz, 4) * 4 + y
                    at = pos_ref[b] - sp * seq_local
                    for i, buf in enumerate((k_buf, v_buf)):
                        new = jnp.zeros((8, 128), F32)
                        for g in range(KV):
                            source = kvs[g, turn, t * 4 + y:t * 4 + y + 1, i * 128:(i + 1) * 128]
                            new = jnp.where(sub % KV == g, source, new)
                        old = buf[b].astype(F32)
                        buf[b] = jnp.concatenate(
                            [jnp.where(sub // KV == at - 2 * v, new, old[v * 8:(v + 1) * 8])
                             for v in range(n_rows // 8)], axis=0).astype(BF16)
            return carry

        lax.fori_loop(0, 4, update, 0)

    def quarter(dx):
        g = lax.rem(group + 4 - dx, KV)
        at = pl.ds(pl.multiple_of(g * quarter_rows, quarter_rows), quarter_rows)
        return g, pltpu.make_async_remote_copy(
            src_ref=full.at[at], dst_ref=other.at[at], send_sem=tp_send.at[g], recv_sem=tp_recv.at[g],
            device_id={"tp": 1 - tp}, device_id_type=MESH)

    def finish(buf, g, core):
        for cb in range(n_cb):
            at = pl.ds(pl.multiple_of((g * 2 + core) * own + cb * 128, 128), 128)
            for t in range(2):
                slab = buf[pl.ds(g * quarter_rows + t * n_cb + cb, n_lines, stride=16), :]
                out_ref[t * 16:(t + 1) * 16, at] = (h_ref[t * 16:(t + 1) * 16, at].astype(F32) + slab).astype(BF16)

    with jax.named_scope("agwait"):
        for dx in QUARTERS:
            g, swap = quarter(dx)
            n = (n_lines if dx else n_lines - 1) * AG_ROWS
            pltpu.make_async_copy(full.at[pl.ds(0, n)], full.at[pl.ds(0, n)], ag_recv.at[g]).wait()
            swap.start()
            finish(full, g, tp)
    with jax.named_scope("swapwait"):
        for dx in QUARTERS:
            g, swap = quarter(dx)
            swap.wait()
            finish(other, g, 1 - tp)

    with jax.named_scope("drain"):
        @pl.when(jnp.logical_and(is_kv, jnp.logical_not(is_last)))
        def _():
            wait_for(4, early_send)

        @pl.when(is_last)
        def _():
            wait_for(3, early_send)

        wait_for_halves(2 * (PLANE - 1), q_send)
        returns = jnp.logical_and(y_at == x_at, jnp.logical_not(is_kv))

        @pl.when(returns)
        def _():
            wait_for(2, late_send)

        @pl.when(jnp.logical_not(returns))
        def _():
            wait_for(3, late_send)

        pltpu.make_async_copy(rs_others, rs_others, rs_send).wait()

        pltpu.make_async_copy(x_others, x_others, x_send).wait()
        f_others = full.at[pl.ds(0, (n_sp - 1) * AG_ROWS)]
        pltpu.make_async_copy(f_others, f_others, ag_send).wait()


def store_kernel(*refs):
    n = len(refs) // 2
    sem = refs[-1]
    copies = [pltpu.make_async_copy(refs[i], refs[n + i], sem.at[i]) for i in range(n)]
    for c in copies:
        c.start()
    for c in copies:
        c.wait()


def solution(mesh):
    cache_spec = P('dp', 'sp', 'tp', None)
    n_sp = mesh.shape["sp"]

    def local_step(hidden, norm_scale, w_qkv, w_out, k_cache, v_cache, positions):
        n_seq, seq_local, kv, head_dim = k_cache.shape
        d_model = hidden.shape[1]
        depth = w_out.shape[0] // kv
        vmem = pl.BlockSpec(memory_space=VMEM)
        hbm = pl.BlockSpec(memory_space=pltpu.HBM)
        half = head_dim // 2
        freq = np.exp(np.arange(half, dtype=np.float32) * np.float32(-2.0 * math.log(500000.0) / head_dim))
        freq = jnp.asarray(np.concatenate([freq, freq])[None].astype(np.float32))
        flat = (n_seq, seq_local * kv, head_dim)
        dma = pltpu.SemaphoreType.DMA

        hidden_type = jax.ShapeDtypeStruct((n_seq, d_model), BF16)
        results = pl.pallas_call(
            step_kernel,
            out_shape=[hidden_type, jax.ShapeDtypeStruct(flat, BF16), jax.ShapeDtypeStruct(flat, BF16)],
            in_specs=[hbm] * 8,
            out_specs=[vmem, vmem, vmem],
            scratch_shapes=[
                pltpu.SMEM((n_seq,), jnp.int32),
                VMEM((n_seq, d_model), BF16),
                VMEM((d_model,), BF16),
                VMEM((1, head_dim), F32),
                dma((4,)),
                VMEM((d_model, head_dim), BF16),
                VMEM((d_model, 2 * head_dim), BF16),
                VMEM((kv // 2, d_model, 4 * head_dim), BF16),
                VMEM((depth, d_model), BF16),
                VMEM((PLANE, 4, 8, head_dim), F32),
                VMEM((kv, 4, 8, 2 * head_dim), F32),
                VMEM((n_seq * 32, head_dim), F32),
                VMEM((n_seq * 32, head_dim), BF16),
                VMEM((n_sp * 16, head_dim), F32),
                VMEM((n_sp * 16, head_dim), F32),
                VMEM((8, depth), F32),
                VMEM((OWNERS * 16, head_dim), F32),
                VMEM((OWNERS * 16, head_dim), F32),
                VMEM((n_sp * 16, head_dim), F32),
                VMEM((n_sp * 16, head_dim), F32),
                dma((K_CHUNKS,)), dma, dma((kv,)), dma((kv,)), dma((2,)), dma, dma((2,)),
            ] + [dma] * 9 + [dma((kv,))] * 3 + [pltpu.SemaphoreType.REGULAR],
            compiler_params=pltpu.CompilerParams(
                collective_id=0, has_side_effects=True, vmem_limit_bytes=48 * 1024 * 1024),
            cost_estimate=pl.CostEstimate(flops=60_000_000_000, bytes_accessed=20_000_000, transcendentals=0),
            name="step",
        )(*[pltpu.with_memory_space_constraint(a, pltpu.HBM) for a in (
            positions, hidden, norm_scale, freq, w_qkv, w_out, k_cache.reshape(flat), v_cache.reshape(flat))])

        h_out, k_new, v_new = pl.pallas_call(
            store_kernel,
            out_shape=[hidden_type, jax.ShapeDtypeStruct(flat, BF16), jax.ShapeDtypeStruct(flat, BF16)],
            in_specs=[vmem] * 3,
            out_specs=[hbm] * 3,
            scratch_shapes=[dma((3,))],
            compiler_params=pltpu.CompilerParams(vmem_limit_bytes=8 * 1024 * 1024),
            name="store",
        )(*[pltpu.with_memory_space_constraint(a, VMEM) for a in results])
        k_new, v_new = k_new.reshape(k_cache.shape), v_new.reshape(v_cache.shape)
        return h_out, k_new, v_new

    return jax.shard_map(
        local_step,
        mesh=mesh,
        in_specs=(P('dp', None), P(None), P(None, 'tp'), P('tp', None), cache_spec, cache_spec, P('dp')),
        out_specs=(P('dp', None), cache_spec, cache_spec),
        check_vma=False,
    )
```

profile of v0, /device:TPU:1, one launch (start us, length us, event | category | flops | bytes accessed | tf_op | source)
XLA Modules:
  0.0 39.3 jit_solution(11780980287360888928)
XLA Ops:
  0.6 36.5 %step.1 = (bf16[32,6144]{1,0:T(8,128)(2,1)S(1)}, bf16[32,256,128]{2,1,0:T(8,128)(2,1)S(1)}, bf16[32,256,128]{2,1,0:T(8,128)(2,1)S(1)}) custom-call(s32[32]{0:T(128)} %pos_hbm.1, bf16[32,6144]{1,0:T(8,128)(2,1)} %h_hbm.1, bf16[6144]{0:T(1024)(128)(2,1)} %scale_hbm.1, f32[1,128]{1,0:T(1,128)} %constant.2.clone.freq_hbm, bf16[6144,4096]{1,0:T(8,128)(2,1)} %wq_ref.1, ...), custom_call_target="tpu_custom_call" | custom-call | flops 60000002048 | bytes 20000000 | tf_op jit(solution)/shard_map/step/pallas_call | solution.py:492
  37.2 2.2 %store.1 = (bf16[32,6144]{1,0:T(8,128)(2,1)}, bf16[32,256,128]{2,1,0:T(8,128)(2,1)}, bf16[32,256,128]{2,1,0:T(8,128)(2,1)}) custom-call(bf16[32,6144]{1,0:T(8,128)(2,1)S(1)} %get-tuple-element.9.refs_0_, bf16[32,256,128]{2,1,0:T(8,128)(2,1)S(1)} %get-tuple-element.10.refs_1_, bf16[32,256,128]{2,1,0:T(8,128)(2,1)S(1)} %get-tuple-element.11.refs_2_), custom_call_target="tpu_custom_call" | custom-call | tf_op jit(solution)/shard_map/store/pallas_call | solution.py:527
where the time goes:
time: 39.5 us; the launch traced here: 39.3 us
  Pallas kernels  38.7 us (98%)
  between operations  0.64 us (2%)
    pallas_call x1, Pallas kernels, local_step(): pl.pallas_call(step_kernel, out_shape=[hidden_type, jax.ShapeDtypeStruct(...  36.5 us
    pallas_call x1, Pallas kernels, local_step(): pl.pallas_call(store_kernel, out_shape=[hidden_type, jax.ShapeDtypeStruct...  2.17 us

commit v1 on v0

--- a/solution.py
+++ b/solution.py
@@ -14,13 +14,14 @@
 F32 = jnp.float32
 BF16 = jnp.bfloat16
 NEG = -3.0e38
+LEAST = -1.0e38
 PLANE = 16
 K_CHUNKS = 6
 KV = 4
 OWNERS = 8
 TURNS = (2, 1, 3, 0)
 QUARTERS = (0, 1, 3, 2)
-RS_ROWS = 14
+RS_ROWS = 13
 AG_ROWS = 12
 
 
@@ -99,6 +100,8 @@
 
     with jax.named_scope("hwait"):
         small[0].wait()
+        for g in range(KV):
+            wl_copy(g).start()
     with jax.named_scope("norm"):
         hidden = h_ref[...].astype(F32)
         centered = hidden - jnp.mean(hidden, axis=-1, keepdims=True)
@@ -106,8 +109,6 @@
     with jax.named_scope("inwait"):
         for c in small[1:]:
             c.wait()
-        for g in range(KV):
-            wl_copy(g).start()
     with jax.named_scope("norm2"):
         u = (centered * lax.rsqrt(var + 1e-5) * scale_ref[...].astype(F32)[None, :]).astype(BF16)
         seq_row = lax.broadcasted_iota(jnp.int32, (n_seq, 128), 0)
@@ -237,16 +238,16 @@
             stats, outs = [], []
             for t in range(2):
                 s = held[i * 2 + t]
-                m = jnp.max(s, axis=1, keepdims=True)
+                m = jnp.maximum(jnp.max(s, axis=1, keepdims=True), LEAST)
                 e = jnp.exp(s - m)
                 stats.append((m, jnp.sum(e, axis=1, keepdims=True)))
                 outs.append(jnp.dot(e.astype(BF16), v_buf[ln + 16 * t], preferred_element_type=F32))
             (m0, l0), (m1, l1) = stats
-            first = jnp.where(row8 == 6, as_rows((m0, m1), KV), jnp.where(row8 == 7, as_rows((l0, l1), KV), outs[0]))
+            first = jnp.where(row8 == 6, as_rows((m0, m1, l0, l1), KV), outs[0])
             for g in range(KV):
                 at = pl.multiple_of((ln * KV + g) * 16, 16)
                 part[pl.ds(at, 8), :] = first[g * 8:(g + 1) * 8]
-                part[pl.ds(at + 8, 8), :] = outs[1][g * 8:(g + 1) * 8]
+                part[pl.ds(at + 7, 6), :] = outs[1][g * 8:g * 8 + 6]
 
     def send_partials(turn):
         for i in range(4):
@@ -301,7 +302,7 @@
     with jax.named_scope("merge"):
         lane = lax.broadcasted_iota(jnp.int32, (1, 128), 1)
         m = parts[pl.ds(6, n_sp, stride=16), :]
-        l = parts[pl.ds(7, n_sp, stride=16), :]
+        l = pltpu.roll(m, 112, 1)
         top = jnp.maximum(jnp.max(m, axis=0, keepdims=True), m_new)
         f = jnp.exp(m - top)
         f_new = jnp.exp(m_new - top)
@@ -313,7 +314,7 @@
             w8 = wt[t * 8:(t + 1) * 8]
             sums = [w8[:, n_sp:n_sp + 1] * v_new[t]] + [jnp.zeros((8, 128), F32)] * 3
             for s in range(n_sp):
-                sums[s % 4] += w8[:, s:s + 1] * parts[s * 16 + t * 8:s * 16 + t * 8 + 8, :]
+                sums[s % 4] += w8[:, s:s + 1] * parts[s * 16 + t * 7:s * 16 + t * 7 + 8, :]
             acc = (sums[0] + sums[1]) + (sums[2] + sums[3])
             for hd in range(6):
                 lhs[t:t + 1, hd * 128:(hd + 1) * 128] = acc[hd:hd + 1, :]

time: 39.5 us -> 39.1 us (0.990)
  no operation moved by 1% of the time
where the time goes in v1:
time: 39.1 us; the launch traced here: 39 us
  Pallas kernels  38.4 us (98%)
  between operations  0.64 us (2%)
    pallas_call x1, Pallas kernels, local_step(): pl.pallas_call(step_kernel, out_shape=[hidden_type, jax.ShapeDtypeStruct(...  36.2 us
    pallas_call x1, Pallas kernels, local_step(): pl.pallas_call(store_kernel, out_shape=[hidden_type, jax.ShapeDtypeStruct...  2.17 us

profile of v1, /device:TPU:1, one launch (start us, length us, event | category | flops | bytes accessed | tf_op | source)
XLA Modules:
  0.0 39.0 jit_solution(3782346005242466599)
XLA Ops:
  0.6 36.2 %step.1 = (bf16[32,6144]{1,0:T(8,128)(2,1)S(1)}, bf16[32,256,128]{2,1,0:T(8,128)(2,1)S(1)}, bf16[32,256,128]{2,1,0:T(8,128)(2,1)S(1)}) custom-call(s32[32]{0:T(128)} %pos_hbm.1, bf16[32,6144]{1,0:T(8,128)(2,1)} %h_hbm.1, bf16[6144]{0:T(1024)(128)(2,1)} %scale_hbm.1, f32[1,128]{1,0:T(1,128)} %constant.2.clone.freq_hbm, bf16[6144,4096]{1,0:T(8,128)(2,1)} %wq_ref.1, ...), custom_call_target="tpu_custom_call" | custom-call | flops 60000002048 | bytes 20000000 | tf_op jit(solution)/shard_map/step/pallas_call | solution.py:493
  36.8 2.2 %store.1 = (bf16[32,6144]{1,0:T(8,128)(2,1)}, bf16[32,256,128]{2,1,0:T(8,128)(2,1)}, bf16[32,256,128]{2,1,0:T(8,128)(2,1)}) custom-call(bf16[32,6144]{1,0:T(8,128)(2,1)S(1)} %get-tuple-element.9.refs_0_, bf16[32,256,128]{2,1,0:T(8,128)(2,1)S(1)} %get-tuple-element.10.refs_1_, bf16[32,256,128]{2,1,0:T(8,128)(2,1)S(1)} %get-tuple-element.11.refs_2_), custom_call_target="tpu_custom_call" | custom-call | tf_op jit(solution)/shard_map/store/pallas_call | solution.py:528

commit v2 on v1

--- a/solution.py
+++ b/solution.py
@@ -156,9 +156,8 @@
 
     is_last = jnp.logical_and(is_kv, y_at == 3)
     with jax.named_scope("qsend"):
-        for half in range(2):
-            for dy, dx in PLANE_ORDER:
-                to_plane(dy, dx, recv.at[j, pl.ds(half * 2, 2)], q_send, q_recv.at[half]).start()
+        for dy, dx in PLANE_ORDER:
+            to_plane(dy, dx, recv.at[j], q_send, q_recv.at[0]).start()
         for dz in range(1, 4):
             pl.semaphore_signal(ready, inc=1, device_id={"sp": lax.rem(sp + dz * PLANE, n_sp)}, device_id_type=MESH)
         for g in range(KV):
@@ -196,7 +195,8 @@
 
     def half_queries(half):
         with jax.named_scope(f"qwait{half}"):
-            wait_for_halves(PLANE - 1, q_recv.at[half])
+            if half == 0:
+                wait_for_halves(2 * (PLANE - 1), q_recv.at[0])
         with jax.named_scope("spread"):
             for turn in (half * 2, half * 2 + 1):
                 for blk in range(PLANE):

time: 39.1 us -> 40.3 us (1.031)
  Pallas kernels: 38.4 us -> 39.6 us
    pallas_call x1, Pallas kernels: 36.2 us -> 37.4 us  [local_step(): pl.pallas_call(step_kernel, out_shape=[hidden_type, jax.ShapeDtypeStruct(...]
where the time goes in v2:
time: 40.3 us; the launch traced here: 40.2 us
  Pallas kernels  39.6 us (98%)
  between operations  0.64 us (2%)
    pallas_call x1, Pallas kernels, local_step(): pl.pallas_call(step_kernel, out_shape=[hidden_type, jax.ShapeDtypeStruct(...  37.4 us
    pallas_call x1, Pallas kernels, local_step(): pl.pallas_call(store_kernel, out_shape=[hidden_type, jax.ShapeDtypeStruct...  2.17 us

profile of v2, /device:TPU:1, one launch (start us, length us, event | category | flops | bytes accessed | tf_op | source)
XLA Modules:
  0.0 40.2 jit_solution(2032766093850193081)
XLA Ops:
  0.6 37.4 %step.1 = (bf16[32,6144]{1,0:T(8,128)(2,1)S(1)}, bf16[32,256,128]{2,1,0:T(8,128)(2,1)S(1)}, bf16[32,256,128]{2,1,0:T(8,128)(2,1)S(1)}) custom-call(s32[32]{0:T(128)} %pos_hbm.1, bf16[32,6144]{1,0:T(8,128)(2,1)} %h_hbm.1, bf16[6144]{0:T(1024)(128)(2,1)} %scale_hbm.1, f32[1,128]{1,0:T(1,128)} %constant.2.clone.freq_hbm, bf16[6144,4096]{1,0:T(8,128)(2,1)} %wq_ref.1, ...), custom_call_target="tpu_custom_call" | custom-call | flops 60000002048 | bytes 20000000 | tf_op jit(solution)/shard_map/step/pallas_call | solution.py:493
  38.0 2.2 %store.1 = (bf16[32,6144]{1,0:T(8,128)(2,1)}, bf16[32,256,128]{2,1,0:T(8,128)(2,1)}, bf16[32,256,128]{2,1,0:T(8,128)(2,1)}) custom-call(bf16[32,6144]{1,0:T(8,128)(2,1)S(1)} %get-tuple-element.9.refs_0_, bf16[32,256,128]{2,1,0:T(8,128)(2,1)S(1)} %get-tuple-element.10.refs_1_, bf16[32,256,128]{2,1,0:T(8,128)(2,1)S(1)} %get-tuple-element.11.refs_2_), custom_call_target="tpu_custom_call" | custom-call | tf_op jit(solution)/shard_map/store/pallas_call | solution.py:528
